TPU v7x, 32 devices: a whole 2x2x4 slice. The times are simulated.
32 devices in a mesh: ep: 4 (over x, core), fsdp: 8 (over z, y).
Axes of the slice: x: 2, y: 2, z: 4, core: 2. Of those that a mesh axis runs over, the one named last changes fastest.
Arguments:
- master_gate: float32 [128, 2048, 768], P('ep', 'fsdp'), may hold values from -0.1875 to 0.1875
- master_up: float32 [128, 2048, 768], P('ep', 'fsdp'), may hold values from -0.1875 to 0.1875
- router_weight: float32 [2048, 128], P('fsdp', 'ep'), may hold values from -0.125 to 0.125
- router_gain: float32 [2048], P('fsdp'), may hold values from 0.25 to 1.75
Outputs:
- final_gate: bfloat16 [128, 2048, 768], P(('ep', 'fsdp'))
- final_up: bfloat16 [128, 2048, 768], P(('ep', 'fsdp'))
- scale_gate: float32 [128, 768], P(('ep', 'fsdp'))
- scale_up: float32 [128, 768], P(('ep', 'fsdp'))
- serve_router: bfloat16 [2048, 128], replicated
All inputs are finite; a program needn't handle non-finite values.
Results may differ from a plain program's by a relative error of at most 0.001.
Values may be sent and summed in bfloat16 or wider, within the bound.
A program may use at most 192 MiB of HBM per device.

v0:
```python
import jax
import jax.numpy as jnp
from jax import lax
from jax.sharding import PartitionSpec as P


def body(master_gate, master_up, router_weight, router_gain):
    total_gate, total_up = lax.psum(
        (jnp.sum(master_gate * master_gate, axis=1), jnp.sum(master_up * master_up, axis=1)), "fsdp"
    )
    scale_gate = jnp.sqrt(total_gate)
    scale_up = jnp.sqrt(total_up)
    narrow_gate, narrow_up = (
        (master_gate / jnp.expand_dims(scale_gate, 1)).astype(jnp.bfloat16),
        (master_up / jnp.expand_dims(scale_up, 1)).astype(jnp.bfloat16),
    )
    final_gate, final_up = (
        lax.all_to_all(narrow_gate, "fsdp", split_axis=0, concat_axis=1, tiled=True),
        lax.all_to_all(narrow_up, "fsdp", split_axis=0, concat_axis=1, tiled=True),
    )
    scale_gate = lax.dynamic_slice_in_dim(
        scale_gate, lax.axis_index("fsdp") * final_gate.shape[0], final_gate.shape[0], axis=0
    )
    scale_up = lax.dynamic_slice_in_dim(
        scale_up, lax.axis_index("fsdp") * final_up.shape[0], final_up.shape[0], axis=0
    )
    part_router = (router_weight * router_gain[:, None]).astype(jnp.bfloat16)
    row_router = lax.all_gather(part_router, "fsdp", axis=0, tiled=True)
    serve_router = lax.all_gather(row_router, "ep", axis=1, tiled=True)
    return (final_gate, final_up, scale_gate, scale_up, serve_router)


def solution(mesh):
    return jax.shard_map(
        body,
        mesh=mesh,
        in_specs=(P("ep", "fsdp", None), P("ep", "fsdp", None), P("fsdp", "ep"), P("fsdp")),
        out_specs=(
            P(("ep", "fsdp"), None, None),
            P(("ep", "fsdp"), None, None),
            P(("ep", "fsdp"), None),
            P(("ep", "fsdp"), None),
            P(),
        ),
        check_vma=False,
    )
```

profile of v0, /device:TPU:0, one launch (start us, length us, event | category | flops | bytes accessed | tf_op | source)
XLA Modules:
  0.0 723.9 jit_solution(15116092223100259474)
XLA Ops:
  7.2 0.0 all-reduce.3.cloned.1.call-start
  7.2 17.3 %multiply_reduce_fusion = (f32[32,768]{1,0:T(8,128)}, f32[32,768]{1,0:T(8,128)}) fusion(f32[32,256,768]{2,1,0:T(8,128)} %param.5, f32[32,256,768]{2,1,0:T(8,128)} %param.4), kind=kLoop, calls=%fused_computation.1 | loop fusion | flops 25116672 | bytes 50528256 | tf_op jit(solution)/shard_map/reduce_sum | solution.py:9
  24.5 0.0 all-reduce.3.cloned.1.call-update
  24.5 73.8 %all-reduce.3.cloned.1.call-done = (f32[32,768]{1,0:T(8,128)}, f32[32,768]{1,0:T(8,128)}) async-done(((f32[32,768]{1,0:T(8,128)}, f32[32,768]{1,0:T(8,128)}), (f32[32,768]{1,0:T(8,128)}, f32[32,768]{1,0:T(8,128)})) %all-reduce.3.cloned.1.call-update) | async-done | bytes 196624 | tf_op jit(solution)/shard_map/psum | solution.py:8
  98.2 0.9 sqrt.6
  99.2 0.0 copy-start
  99.2 13.7 %divide_convert_fusion.1 = bf16[32,256,768]{2,1,0:T(8,128)(2,1)} fusion(f32[32,256,768]{2,1,0:T(8,128)} %param.4, f32[32,768]{1,0:T(8,128)S(1)} %sqrt.6), kind=kLoop, calls=%fused_computation.2 | loop fusion | flops 12582912 | bytes 37847040 | tf_op jit(solution)/shard_map/convert_element_type | solution.py:14
  112.9 5.4 all-to-all-start
  118.2 0.0 copy-done
  118.3 0.0 copy-start.1
  118.3 0.0 copy-start.2
  118.3 13.8 %divide_convert_fusion = bf16[32,256,768]{2,1,0:T(8,128)(2,1)} fusion(f32[32,256,768]{2,1,0:T(8,128)} %param.5, f32[32,768]{1,0:T(8,128)S(1)} %sqrt.7), kind=kLoop, calls=%fused_computation | loop fusion | flops 12582912 | bytes 37847040 | tf_op jit(solution)/shard_map/convert_element_type | solution.py:15
  132.1 257.3 %all-to-all-done = bf16[32,256,768]{2,1,0:T(8,128)(2,1)} async-done(((bf16[32,256,768]{2,1,0:T(8,128)(2,1)}), bf16[32,256,768]{2,1,0:T(8,128)(2,1)}, u32[]{:S(2)}, u32[]{:S(2)}) %all-to-all-start) | async-done | bytes 12582944 | tf_op jit(solution)/shard_map/all_to_all | solution.py:18
  389.4 5.4 all-to-all-start.1
  394.8 0.0 copy-done.1
  394.8 0.0 copy-done.2
  394.8 291.6 %all_gather.6 = bf16[2048,32]{0,1:T(8,128)(2,1)S(1)} all-gather(bf16[256,32]{0,1:T(8,128)(2,1)S(1)} %multiply_convert_fusion), channel_id=1, replica_groups=mesh['ep'=4,'fsdp'=8] {'fsdp'}, dimensions={0}, use_global_device_ids=true | all-gather | bytes 147456 | tf_op jit(solution)/shard_map/all_gather | solution.py:28
  686.4 7.1 all_gather.7
  693.5 1.0 copy.14
  694.5 0.6 constant_dynamic-slice_fusion
  695.1 0.6 constant_dynamic-slice_fusion.1
  695.7 10.7 %copy.12 = bf16[8,4,256,768]{3,2,0,1:T(8,128)(2,1)} copy(bf16[8,4,256,768]{3,2,1,0:T(8,128)(2,1)} %bitcast) | data formatting | bytes 25165824 | tf_op jit(solution)/shard_map/all_to_all | solution.py:18
  706.4 0.0 all-to-all-done.1
  706.4 10.7 %copy.13 = bf16[8,4,256,768]{3,2,0,1:T(8,128)(2,1)} copy(bf16[8,4,256,768]{3,2,1,0:T(8,128)(2,1)} %bitcast.3) | data formatting | bytes 25165824 | tf_op jit(solution)/shard_map/all_to_all | solution.py:19
  (2 shorter events, 0.0 us)
Async XLA Ops:
  7.2 91.1 %all-reduce.3.cloned.1.call-start = ((), (), s32[]{:S(2)}) async-start(), calls=%async_computation.2 | async-start | bytes 393216 | tf_op jit(solution)/shard_map/psum | solution.py:8
  99.2 19.1 %copy-start = (f32[32,768]{1,0:T(8,128)S(1)}, f32[32,768]{1,0:T(8,128)}, u32[]{:S(2)}) copy-start(f32[32,768]{1,0:T(8,128)} %get-tuple-element.11) | copy-start | bytes 294916
  112.9 276.5 %all-to-all-start = ((bf16[32,256,768]{2,1,0:T(8,128)(2,1)}), bf16[32,256,768]{2,1,0:T(8,128)(2,1)}, u32[]{:S(2)}, u32[]{:S(2)}) async-start(bf16[32,256,768]{2,1,0:T(8,128)(2,1)} %divide_convert_fusion.1), calls=%async_computation | async-start | bytes 25165824 | tf_op jit(solution)/shard_map/all_to_all | solution.py:18
  118.3 276.5 %copy-start.1 = (f32[256,32]{0,1:T(8,128)S(1)}, f32[256,32]{0,1:T(8,128)}, u32[]{:S(2)}) copy-start(f32[256,32]{0,1:T(8,128)} %param.6) | copy-start | bytes 98308
  118.3 276.5 %copy-start.2 = (f32[256]{0:T(256)S(1)}, f32[256]{0:T(256)}, u32[]{:S(2)}) copy-start(f32[256]{0:T(256)} %param.7) | copy-start | bytes 3076
  389.4 317.0 %all-to-all-start.1 = ((bf16[32,256,768]{2,1,0:T(8,128)(2,1)}), bf16[32,256,768]{2,1,0:T(8,128)(2,1)}, u32[]{:S(2)}, u32[]{:S(2)}) async-start(bf16[32,256,768]{2,1,0:T(8,128)(2,1)} %divide_convert_fusion), calls=%async_computation.1 | async-start | bytes 25165824 | tf_op jit(solution)/shard_map/all_to_all | solution.py:19
Sparse Core Ops, SparseCore 0:
  24.6 73.5 all-reduce.2
where the time goes:
time: 724 us
  waiting for transfers between devices  331 us (46%)
  blocking collectives  299 us (41%)
  other arithmetic  44.7 us (6%)
  local copies, waits for them, and re-layouts  24.5 us (3%)
  between operations  14.1 us (2%)
  starting transfers between devices  10.8 us (1%)
    all_gather x1, blocking collectives, body(): row_router = lax.all_gather(part_router, 'fsdp', axis=0, tiled=True)  292 us
    all_to_all x1, waiting for transfers between devices, body(): lax.all_to_all(narrow_gate, 'fsdp', split_axis=0, concat_axis=1, tiled=True)  257 us
    psum x1, waiting for transfers between devices, body(): lax.psum((jnp.sum(master_gate * master_gate, axis=1), jnp.sum(master_up *...  73.8 us
    reduce_sum x1, other arithmetic, body(): jnp.sum(master_up * master_up, axis=1)  17.3 us
  transfers between devices with their start and end apart: 3, of which 2 were waited for; matrix products, arithmetic and copies ran while one was open for 4% of the time, Pallas kernels for 0%

commit v1 on v0

--- a/solution.py
+++ b/solution.py
@@ -1,7 +1,27 @@
+import functools
 import jax
 import jax.numpy as jnp
 from jax import lax
 from jax.sharding import PartitionSpec as P
+
+
+def watch_yards(chunk, dim_k):
+    world = lax.axis_size("fsdp")
+    vals = [chunk]
+    for k in range(world - 1):
+        vals.append(
+            lax.ppermute(
+                vals[-1], axis_name="fsdp", perm=[(idx, (idx + 1) % world) for idx in range(world)]
+            )
+        )
+    return jnp.roll(
+        jnp.concatenate(vals[::-1], axis=dim_k),
+        (lax.axis_index("fsdp") + 1) * chunk.shape[dim_k],
+        axis=dim_k,
+    )
+
+
+lead_loops = functools.partial(watch_yards, dim_k=0)
 
 
 def body(master_gate, master_up, router_weight, router_gain):
@@ -25,7 +45,7 @@
         scale_up, lax.axis_index("fsdp") * final_up.shape[0], final_up.shape[0], axis=0
     )
     part_router = (router_weight * router_gain[:, None]).astype(jnp.bfloat16)
-    row_router = lax.all_gather(part_router, "fsdp", axis=0, tiled=True)
+    row_router = lead_loops(part_router)
     serve_router = lax.all_gather(row_router, "ep", axis=1, tiled=True)
     return (final_gate, final_up, scale_gate, scale_up, serve_router)
 

time: 724 us -> 730 us (level)
  blocking collectives: 299 us -> 7.15 us
  waiting for transfers between devices: 331 us -> 565 us
  starting transfers between devices: 10.8 us -> 73.9 us
    all_gather x1 -> x0, blocking collectives: 292 us -> none  [body(): row_router = lax.all_gather(part_router, 'fsdp', axis=0, tiled=True)]
    ppermute x0 -> x7, waiting for transfers between devices: none -> 234 us  [watch_yards(): lax.ppermute(vals[-1], axis_name='fsdp', perm=[(idx, (idx + 1) % world) f...]
    ppermute x0 -> x7, starting transfers between devices: none -> 63.1 us  [watch_yards(): lax.ppermute(vals[-1], axis_name='fsdp', perm=[(idx, (idx + 1) % world) f...]
  transfers between devices with their start and end apart: 3 -> 10, of which waited for: 2 -> 9; matrix products, arithmetic and copies ran while one was open for 4% -> 4% of each run, Pallas kernels for 0% -> 0%
where the time goes in v1:
time: 730 us
  waiting for transfers between devices  565 us (77%)
  starting transfers between devices  73.9 us (10%)
  other arithmetic  44.8 us (6%)
  local copies, waits for them, and re-layouts  24.6 us (3%)
  between operations  14.2 us (2%)
    all_to_all x1, waiting for transfers between devices, body(): lax.all_to_all(narrow_gate, 'fsdp', split_axis=0, concat_axis=1, tiled=True)  257 us
    ppermute x7, waiting for transfers between devices, watch_yards(): lax.ppermute(vals[-1], axis_name='fsdp', perm=[(idx, (idx + 1) % world) f...  234 us
    psum x1, waiting for transfers between devices, body(): lax.psum((jnp.sum(master_gate * master_gate, axis=1), jnp.sum(master_up *...  73.8 us
    ppermute x7, starting transfers between devices, watch_yards(): lax.ppermute(vals[-1], axis_name='fsdp', perm=[(idx, (idx + 1) % world) f...  63.1 us
    reduce_sum x1, other arithmetic, body(): jnp.sum(master_up * master_up, axis=1)  17.3 us
  transfers between devices with their start and end apart: 10, of which 9 were waited for; matrix products, arithmetic and copies ran while one was open for 4% of the time, Pallas kernels for 0%

profile of v1, /device:TPU:0, one launch (start us, length us, event | category | flops | bytes accessed | tf_op | source)
XLA Modules:
  0.0 729.9 jit_solution(6185651986433440676)
XLA Ops:
  7.2 0.0 all-reduce.3.cloned.1.call-start
  7.2 17.3 %multiply_reduce_fusion = (f32[32,768]{1,0:T(8,128)}, f32[32,768]{1,0:T(8,128)}) fusion(f32[32,256,768]{2,1,0:T(8,128)} %param.5, f32[32,256,768]{2,1,0:T(8,128)} %param.4), kind=kLoop, calls=%fused_computation.1 | loop fusion | flops 25116672 | bytes 50528256 | tf_op jit(solution)/shard_map/reduce_sum | solution.py:29
  24.5 0.0 all-reduce.3.cloned.1.call-update
  24.5 73.8 %all-reduce.3.cloned.1.call-done = (f32[32,768]{1,0:T(8,128)}, f32[32,768]{1,0:T(8,128)}) async-done(((f32[32,768]{1,0:T(8,128)}, f32[32,768]{1,0:T(8,128)}), (f32[32,768]{1,0:T(8,128)}, f32[32,768]{1,0:T(8,128)})) %all-reduce.3.cloned.1.call-update) | async-done | bytes 196624 | tf_op jit(solution)/shard_map/psum | solution.py:28
  98.2 0.9 sqrt.6
  99.2 0.0 copy-start.1
  99.2 13.7 %divide_convert_fusion.1 = bf16[32,256,768]{2,1,0:T(8,128)(2,1)} fusion(f32[32,256,768]{2,1,0:T(8,128)} %param.4, f32[32,768]{1,0:T(8,128)S(1)} %sqrt.6), kind=kLoop, calls=%fused_computation.2 | loop fusion | flops 12582912 | bytes 37847040 | tf_op jit(solution)/shard_map/convert_element_type | solution.py:34
  112.9 5.3 all-to-all-start
  118.2 0.0 copy-done.1
  118.2 0.0 copy-start
  118.3 0.0 copy-start.2
  118.3 13.9 %divide_convert_fusion = bf16[32,256,768]{2,1,0:T(8,128)(2,1)} fusion(f32[32,256,768]{2,1,0:T(8,128)} %param.5, f32[32,768]{1,0:T(8,128)S(1)} %sqrt.7), kind=kLoop, calls=%fused_computation | loop fusion | flops 12582912 | bytes 37847040 | tf_op jit(solution)/shard_map/convert_element_type | solution.py:35
  132.1 257.2 %all-to-all-done = bf16[32,256,768]{2,1,0:T(8,128)(2,1)} async-done(((bf16[32,256,768]{2,1,0:T(8,128)(2,1)}), bf16[32,256,768]{2,1,0:T(8,128)(2,1)}, u32[]{:S(2)}, u32[]{:S(2)}) %all-to-all-start) | async-done | bytes 12582944 | tf_op jit(solution)/shard_map/all_to_all | solution.py:38
  389.4 5.3 all-to-all-start.1
  394.7 0.0 copy-done
  394.7 0.0 copy-done.2
  394.8 1.9 collective-permute-start
  396.7 204.3 %collective-permute-done = bf16[256,32]{0,1:T(8,128)(2,1)S(1)} collective-permute-done((bf16[256,32]{0,1:T(8,128)(2,1)S(1)}, bf16[256,32]{0,1:T(8,128)(2,1)S(1)}, u32[]{:S(2)}, u32[]{:S(2)}) %collective-permute-start) | collective-permute-done | bytes 16416 | tf_op jit(solution)/shard_map/ppermute | solution.py:13
  601.0 0.0 collective-permute-start.1
  601.0 6.5 collective-permute-done.1
  607.5 24.0 %collective-permute-start.2 = (bf16[256,32]{0,1:T(8,128)(2,1)S(1)}, bf16[256,32]{0,1:T(8,128)(2,1)S(1)}, u32[]{:S(2)}, u32[]{:S(2)}) collective-permute-start(bf16[256,32]{0,1:T(8,128)(2,1)S(1)} %collective-permute-done.1), channel_id=1, source_target_pairs={{0,1},{1,2},{2,3},{3,4},{4,5},{5,6},{6,7},{7,0},{8,9},{9,10},{10,1... | collective-permute-start | bytes 49160 | tf_op jit(solution)/shard_map/ppermute | solution.py:13
  631.5 6.7 collective-permute-done.2
  638.2 32.7 %collective-permute-start.3 = (bf16[256,32]{0,1:T(8,128)(2,1)S(1)}, bf16[256,32]{0,1:T(8,128)(2,1)S(1)}, u32[]{:S(2)}, u32[]{:S(2)}) collective-permute-start(bf16[256,32]{0,1:T(8,128)(2,1)S(1)} %collective-permute-done.2), channel_id=1, source_target_pairs={{0,1},{1,2},{2,3},{3,4},{4,5},{5,6},{6,7},{7,0},{8,9},{9,10},{10,1... | collective-permute-start | bytes 49160 | tf_op jit(solution)/shard_map/ppermute | solution.py:13
  670.9 1.4 collective-permute-done.3
  672.4 3.4 collective-permute-start.4
  675.8 3.5 collective-permute-done.4
  679.3 1.1 collective-permute-start.5
  680.4 5.3 collective-permute-done.5
  685.7 0.0 collective-permute-start.6
  685.7 6.4 collective-permute-done.6
  692.3 7.1 all_gather.3
  699.5 1.0 copy.14
  700.5 0.6 constant_dynamic-slice_fusion.2
  701.1 0.6 constant_dynamic-slice_fusion.1
  701.7 10.7 %copy.12 = bf16[8,4,256,768]{3,2,0,1:T(8,128)(2,1)} copy(bf16[8,4,256,768]{3,2,1,0:T(8,128)(2,1)} %bitcast) | data formatting | bytes 25165824 | tf_op jit(solution)/shard_map/all_to_all | solution.py:38
  712.4 0.0 all-to-all-done.1
  712.4 10.7 %copy.13 = bf16[8,4,256,768]{3,2,0,1:T(8,128)(2,1)} copy(bf16[8,4,256,768]{3,2,1,0:T(8,128)(2,1)} %bitcast.3) | data formatting | bytes 25165824 | tf_op jit(solution)/shard_map/all_to_all | solution.py:39
  (19 shorter events, 0.1 us)
Async XLA Ops:
  7.2 91.1 %all-reduce.3.cloned.1.call-start = ((), (), s32[]{:S(2)}) async-start(), calls=%async_computation.2 | async-start | bytes 393216 | tf_op jit(solution)/shard_map/psum | solution.py:28
  99.2 19.0 %copy-start.1 = (f32[32,768]{1,0:T(8,128)S(1)}, f32[32,768]{1,0:T(8,128)}, u32[]{:S(2)}) copy-start(f32[32,768]{1,0:T(8,128)} %get-tuple-element.11) | copy-start | bytes 294916
  112.9 276.5 %all-to-all-start = ((bf16[32,256,768]{2,1,0:T(8,128)(2,1)}), bf16[32,256,768]{2,1,0:T(8,128)(2,1)}, u32[]{:S(2)}, u32[]{:S(2)}) async-start(bf16[32,256,768]{2,1,0:T(8,128)(2,1)} %divide_convert_fusion.1), calls=%async_computation | async-start | bytes 25165824 | tf_op jit(solution)/shard_map/all_to_all | solution.py:38
  118.2 276.5 %copy-start = (f32[256,32]{0,1:T(8,128)S(1)}, f32[256,32]{0,1:T(8,128)}, u32[]{:S(2)}) copy-start(f32[256,32]{0,1:T(8,128)} %param.6) | copy-start | bytes 98308
  118.3 276.5 %copy-start.2 = (f32[256]{0:T(256)S(1)}, f32[256]{0:T(256)}, u32[]{:S(2)}) copy-start(f32[256]{0:T(256)} %param.7) | copy-start | bytes 3076
  389.4 323.0 %all-to-all-start.1 = ((bf16[32,256,768]{2,1,0:T(8,128)(2,1)}), bf16[32,256,768]{2,1,0:T(8,128)(2,1)}, u32[]{:S(2)}, u32[]{:S(2)}) async-start(bf16[32,256,768]{2,1,0:T(8,128)(2,1)} %divide_convert_fusion), calls=%async_computation.1 | async-start | bytes 25165824 | tf_op jit(solution)/shard_map/all_to_all | solution.py:39
  394.8 206.2 %collective-permute-start = (bf16[256,32]{0,1:T(8,128)(2,1)S(1)}, bf16[256,32]{0,1:T(8,128)(2,1)S(1)}, u32[]{:S(2)}, u32[]{:S(2)}) collective-permute-start(bf16[256,32]{0,1:T(8,128)(2,1)S(1)} %multiply_convert_fusion), channel_id=1, source_target_pairs={{0,1},{1,2},{2,3},{3,4},{4,5},{5,6},{6,7},{7,0},{8,9},{9,10},{10,1... | collective-permute-start | bytes 49160 | tf_op jit(solution)/shard_map/ppermute | solution.py:13
  601.0 6.5 collective-permute-start.1
  607.5 30.7 %collective-permute-start.2 = (bf16[256,32]{0,1:T(8,128)(2,1)S(1)}, bf16[256,32]{0,1:T(8,128)(2,1)S(1)}, u32[]{:S(2)}, u32[]{:S(2)}) collective-permute-start(bf16[256,32]{0,1:T(8,128)(2,1)S(1)} %collective-permute-done.1), channel_id=1, source_target_pairs={{0,1},{1,2},{2,3},{3,4},{4,5},{5,6},{6,7},{7,0},{8,9},{9,10},{10,1... | collective-permute-start | bytes 49160 | tf_op jit(solution)/shard_map/ppermute | solution.py:13
  638.2 34.1 %collective-permute-start.3 = (bf16[256,32]{0,1:T(8,128)(2,1)S(1)}, bf16[256,32]{0,1:T(8,128)(2,1)S(1)}, u32[]{:S(2)}, u32[]{:S(2)}) collective-permute-start(bf16[256,32]{0,1:T(8,128)(2,1)S(1)} %collective-permute-done.2), channel_id=1, source_target_pairs={{0,1},{1,2},{2,3},{3,4},{4,5},{5,6},{6,7},{7,0},{8,9},{9,10},{10,1... | collective-permute-start | bytes 49160 | tf_op jit(solution)/shard_map/ppermute | solution.py:13
  672.4 6.9 collective-permute-start.4
  679.3 6.4 collective-permute-start.5
  685.7 6.4 collective-permute-start.6
Sparse Core Ops, SparseCore 0:
  24.6 73.5 all-reduce.2
